TPU v7x, 128 devices: a whole 4x4x4 slice. The times are simulated.
128 devices in a mesh: dp: 16 (over y_hi, x, core), tensor: 8 (over z, y_lo).
Axes of the slice: x: 4, y: 4 (y_hi: 2, y_lo: 2; y = y_hi * 2 + y_lo), z: 4, core: 2. Of those that a mesh axis runs over, the one named last changes fastest.
Arguments:
- tokens: bfloat16 [32768, 1024], P(('dp', 'tensor')), may hold values from -6 to 6
- upstream: bfloat16 [32768, 1024], P(('dp', 'tensor')), may hold values from -6 to 6
- counts: int32 [512], P('dp'), may hold values from 37 to 49, as said below
- norm_gain: float32 [1024], replicated, may hold values from 0.5 to 1.5
- norm_bias: float32 [1024], replicated, may hold values from -4 to 4
- w_qkv: bfloat16 [1024, 3072], P('dp', 'tensor'), may hold values from -0.1875 to 0.1875
- w_out: bfloat16 [1024, 1024], P('tensor', 'dp'), may hold values from -0.1875 to 0.1875
Outputs:
- grad_tokens: bfloat16 [32768, 1024], P(('dp', 'tensor'))
- grad_qkv: float32 [1024, 3072], P('dp', 'tensor')
- grad_out: float32 [1024, 1024], P('tensor', 'dp')
- grad_gain: float32 [1024], replicated
- grad_bias: float32 [1024], replicated
Inputs may be any that keep to these rules, and one draw needn't show every extreme that they name: counts[i] is the number of visible tokens of image i, held in its first slots; some image has 49 in every draw.
All inputs are finite; a program needn't handle non-finite values.
Results may differ from a plain program's by a relative error of at most 0.014.
Values may be sent and summed in bfloat16 or wider, within the bound.
A program may use at most 64 MiB of HBM per device.

v0:
```python
import functools

import jax
import jax.numpy as jnp
from jax import lax
from jax.sharding import Mesh
from jax.sharding import PartitionSpec as P

HEAD = 64
CAP = 64
TENSOR = ("tensor_0", "tensor_1")
DP = ("dp_0", "dp_1", "dp_2")
DP_TENSOR = ("dp_0", "dp_1", "dp_2", "tensor_0", "tensor_1")


def laid_out(pieces, dim):
    pieces = jnp.moveaxis(pieces, 0, dim)
    lengths = pieces.shape
    return pieces.reshape(*lengths[:dim], lengths[dim] * lengths[dim + 1], *lengths[dim + 2 :])


def sent_to_all(value, axis):
    copies = jnp.broadcast_to(value, (lax.axis_size(axis), *value.shape))
    return lax.all_to_all(copies, axis, split_axis=0, concat_axis=0, tiled=True)


def gather_directly(value, axis, dim):
    return laid_out(sent_to_all(value, axis), dim)


def in_blocks(value, dim, devices):
    before, after = (value.shape[:dim], value.shape[dim + 1 :])
    return jnp.moveaxis(value.reshape(*before, devices, -1, *after), dim, 0)


def summed_on_arrival(value, axis, dim):
    pieces = in_blocks(value, dim, lax.axis_size(axis))
    arrived = lax.all_to_all(pieces, axis, split_axis=0, concat_axis=0, tiled=True)
    return arrived.astype(jnp.float32).sum(axis=0)


def by_axis(value, axes):
    return functools.reduce(lax.psum, axes, value)


def layer_norm(tokens, norm_gain, norm_bias):
    values = tokens.astype(jnp.float32)
    centre = jnp.mean(values, axis=-1, keepdims=True)
    shifted = values - centre
    variance = jnp.mean(shifted * shifted, axis=-1, keepdims=True)
    inverse_std = lax.rsqrt(variance + 1e-06)
    scaled = shifted * inverse_std
    normed = (scaled * norm_gain + norm_bias).astype(jnp.bfloat16)
    return (normed, scaled, inverse_std)


def on_device(tokens, upstream, counts, norm_gain, norm_bias, w_qkv, w_out):
    local_rows = tokens.shape[0]
    own_images = local_rows // CAP
    start_image = lax.axis_index(TENSOR) * own_images
    own_counts = lax.dynamic_slice_in_dim(counts, start_image, own_images)
    own_live = (
        (jnp.arange(CAP, dtype=jnp.int32)[None, :] < own_counts[:, None])
        .reshape(-1)
        .astype(jnp.float32)
    )
    normed, scaled, inverse_std = layer_norm(tokens, norm_gain, norm_bias)
    all_normed = gather_directly(normed, TENSOR, 0)
    qkv_cols = gather_directly(w_qkv, DP, 0)
    out_rows = gather_directly(w_out, DP, 1)
    all_upstream = gather_directly(upstream, TENSOR, 0)
    group_rows = all_normed.shape[0]
    images = group_rows // CAP
    local_heads = qkv_cols.shape[1] // (3 * HEAD)
    slot_live = jnp.arange(CAP, dtype=jnp.int32)[None, :] < counts[:, None]
    group_live = slot_live.reshape(-1).astype(jnp.bfloat16)
    masked = all_upstream * group_live[:, None]
    projected = jnp.dot(all_normed, qkv_cols, preferred_element_type=jnp.float32).astype(
        jnp.bfloat16
    )
    projected = projected.reshape(images, CAP, local_heads, 3, HEAD)
    query_rows = projected[:, :, :, 0]
    key_rows = projected[:, :, :, 1]
    value_rows = projected[:, :, :, 2]
    score_scale = 1.0 / HEAD**0.5
    scores = (
        jnp.einsum("bqhe,bkhe->bhqk", query_rows, key_rows, preferred_element_type=jnp.float32)
        * score_scale
    )
    scores = jnp.where(slot_live[:, None, None, :], scores, -1e30)
    probs = jax.nn.softmax(scores, axis=-1)
    probs_low = probs.astype(jnp.bfloat16)
    attended = jnp.einsum(
        "bhqk,bkhe->bqhe", probs_low, value_rows, preferred_element_type=jnp.float32
    )
    attended = attended.astype(jnp.bfloat16).reshape(group_rows, local_heads * HEAD)
    out_part = lax.dot_general(
        attended, masked, (((0,), (0,)), ((), ())), preferred_element_type=jnp.float32
    )
    grad_out = summed_on_arrival(out_part.astype(jnp.bfloat16), DP, 1)
    grad_att = lax.dot_general(
        masked, out_rows, (((1,), (1,)), ((), ())), preferred_element_type=jnp.float32
    )
    grad_att = grad_att.astype(jnp.bfloat16).reshape(images, CAP, local_heads, HEAD)
    grad_probs = jnp.einsum(
        "bqhe,bkhe->bhqk", grad_att, value_rows, preferred_element_type=jnp.float32
    )
    row_delta = jnp.sum(probs * grad_probs, axis=-1, keepdims=True)
    grad_scores = (probs * (grad_probs - row_delta) * score_scale).astype(jnp.bfloat16)
    grad_value = jnp.einsum(
        "bhqk,bqhe->bkhe", probs_low, grad_att, preferred_element_type=jnp.float32
    ).astype(jnp.bfloat16)
    grad_query = jnp.einsum(
        "bhqk,bkhe->bqhe", grad_scores, key_rows, preferred_element_type=jnp.float32
    ).astype(jnp.bfloat16)
    grad_key = jnp.einsum(
        "bhqk,bqhe->bkhe", grad_scores, query_rows, preferred_element_type=jnp.float32
    ).astype(jnp.bfloat16)
    grad_proj = jnp.stack([grad_query, grad_key, grad_value], axis=3).reshape(
        group_rows, 3 * local_heads * HEAD
    )
    qkv_part = lax.dot_general(
        all_normed, grad_proj, (((0,), (0,)), ((), ())), preferred_element_type=jnp.float32
    )
    grad_qkv = summed_on_arrival(qkv_part.astype(jnp.bfloat16), DP, 0)
    grad_normed = lax.psum_scatter(
        lax.dot_general(
            grad_proj, qkv_cols, (((1,), (1,)), ((), ())), preferred_element_type=jnp.float32
        ).astype(jnp.bfloat16),
        TENSOR,
        scatter_dimension=0,
        tiled=True,
    ).astype(jnp.float32)
    grad_gain, grad_bias = (
        by_axis(jnp.sum(grad_normed * scaled, axis=0), DP_TENSOR),
        by_axis(jnp.sum(grad_normed, axis=0), DP_TENSOR),
    )
    grad_scaled = grad_normed * norm_gain
    grad_ln = inverse_std * (
        grad_scaled
        - jnp.mean(grad_scaled, axis=-1, keepdims=True)
        - scaled * jnp.mean(grad_scaled * scaled, axis=-1, keepdims=True)
    )
    grad_tokens = (upstream.astype(jnp.float32) * own_live[:, None] + grad_ln).astype(jnp.bfloat16)
    return (grad_tokens, grad_qkv, grad_out, grad_gain, grad_bias)


def solution(mesh):
    finer = Mesh(
        mesh.devices.reshape(2, 4, 2, 4, 2), ("dp_0", "dp_1", "dp_2", "tensor_0", "tensor_1")
    )
    in_specs = (
        P(DP_TENSOR, None),
        P(DP_TENSOR, None),
        P(DP),
        P(),
        P(),
        P(DP, TENSOR),
        P(TENSOR, DP),
    )
    out_specs = (P(DP_TENSOR, None), P(DP, TENSOR), P(TENSOR, DP), P(), P())
    return jax.shard_map(
        on_device, mesh=finer, in_specs=in_specs, out_specs=out_specs, check_vma=False
    )
```

profile of v0, /device:TPU:1, one launch (start us, length us, event | category | flops | bytes accessed | tf_op | source)
XLA Modules:
  0.0 362.0 jit_solution(6722173262081360029)
XLA Ops:
  8.0 16.9 %all_to_all.30 = bf16[16,128,64]{1,2,0:T(8,128)(2,1)S(1)} all-to-all(bf16[16,128,64]{1,2,0:T(8,128)(2,1)S(1)} %broadcast_in_dim.25), channel_id=1, replica_groups=mesh['dp_0'=2,'dp_1'=4,'dp_2'=2,'tensor_0'=4,'tensor_1'=2] {'dp_0','dp_1..., dimensions={0} | all-to-all | bytes 524288 | tf_op jit(solution)/shard_map/all_to_all | solution.py:24
  25.8 18.2 %all_to_all.31 = bf16[16,64,384]{2,1,0:T(8,128)(2,1)} all-to-all(bf16[16,64,384]{2,1,0:T(8,128)(2,1)S(1)} %broadcast_in_dim.17), channel_id=1, replica_groups=mesh['dp_0'=2,'dp_1'=4,'dp_2'=2,'tensor_0'=4,'tensor_1'=2] {'dp_0','dp_1..., dimensions={0} | all-to-all | bytes 1572864 | tf_op jit(solution)/shard_map/all_to_all | solution.py:24
  44.1 2.5 broadcast_in_dim.24
  46.6 5.3 %all-to-all-start.2 = ((bf16[8,256,1024]{2,1,0:T(8,128)(2,1)}), bf16[8,256,1024]{2,1,0:T(8,128)(2,1)}, u32[]{:S(2)}, u32[]{:S(2)}) async-start(bf16[8,256,1024]{2,1,0:T(8,128)(2,1)} %broadcast_in_dim.24), calls=%async_computation.2 | async-start | bytes 8388608 | tf_op jit(solution)/shard_map/all_to_all | solution.py:24
  52.6 47.8 %all-to-all-done.2 = bf16[8,256,1024]{2,1,0:T(8,128)(2,1)} async-done(((bf16[8,256,1024]{2,1,0:T(8,128)(2,1)}), bf16[8,256,1024]{2,1,0:T(8,128)(2,1)}, u32[]{:S(2)}, u32[]{:S(2)}) %all-to-all-start.2) | async-done | bytes 4194336 | tf_op jit(solution)/shard_map/all_to_all | solution.py:24
  100.4 2.5 broadcast_in_dim.16
  103.0 4.7 %all-to-all-start = ((bf16[8,256,1024]{2,1,0:T(8,128)(2,1)}), bf16[8,256,1024]{2,1,0:T(8,128)(2,1)}, u32[]{:S(2)}, u32[]{:S(2)}) async-start(bf16[8,256,1024]{2,1,0:T(8,128)(2,1)} %broadcast_in_dim.16), calls=%async_computation | async-start | bytes 8388608 | tf_op jit(solution)/shard_map/all_to_all | solution.py:24
  108.1 2.5 broadcast_multiply_fusion
  116.4 38.9 %all-to-all-done = bf16[8,256,1024]{2,1,0:T(8,128)(2,1)} async-done(((bf16[8,256,1024]{2,1,0:T(8,128)(2,1)}), bf16[8,256,1024]{2,1,0:T(8,128)(2,1)}, u32[]{:S(2)}, u32[]{:S(2)}) %all-to-all-start) | async-done | bytes 4194336 | tf_op jit(solution)/shard_map/all_to_all | solution.py:24
  155.3 4.7 %convolution_convert_fusion.1 = bf16[2048,384]{1,0:T(8,128)(2,1)S(1)} fusion(bf16[2048,1024]{1,0:T(8,128)(2,1)} %bitcast, bf16[1024,384]{1,0:T(8,128)(2,1)} %bitcast.74), kind=kOutput, calls=%fused_computation.4 | convolution fusion | flops 1611399168 | bytes 6553600 | tf_op jit(solution)/shard_map/dot_general | solution.py:78
  160.1 4.8 %reshape.134 = bf16[32,64,2,3,64]{4,3,2,1,0:T(4,128)(2,1)} reshape(bf16[2048,384]{1,0:T(8,128)(2,1)S(1)} %convolution_convert_fusion.1) | data formatting | bytes 3145728 | tf_op jit(solution)/shard_map/reshape | solution.py:81
  164.8 12.1 %fusion.58 = (bf16[32,64,2,1,64]{4,3,2,1,0:T(2,128)(2,1)S(1)}, bf16[32,64,2,1,64]{4,3,2,1,0:T(2,128)(2,1)}, bf16[32,64,2,1,64]{4,3,2,1,0:T(2,128)(2,1)}) fusion(bf16[32,64,2,3,64]{4,3,2,1,0:T(4,128)(2,1)} %reshape.134), kind=kLoop, calls=%fused_computation.75 | loop fusion | bytes 3145728 | tf_op jit(solution)/shard_map/slice | solution.py:84
  178.8 4.8 %fusion.59 = (f32[32,2,64]{2,1,0:T(2,128)S(1)}, f32[32,2,64,64]{2,3,1,0:T(8,128)}) fusion(pred[32,64]{1,0:T(8,128)(4,1)S(1)} %iota_compare_fusion, bf16[32,64,2,1,64]{4,3,2,1,0:T(2,128)(2,1)} %get-tuple-element.21, bf16[32,64,2,1,64]{4,3,2,1,0:T(2,128)(2,1)} %get-tuple-element.20), kind=kOutput, calls=%fused_computation.76 | convolution fusion | flops 34603072 | bytes 2115584 | tf_op jit(solution)/shard_map/sub | solution.py:91
  183.6 3.6 fusion.21
  187.2 6.1 %fusion.23 = bf16[32,64,2,1,64]{1,4,2,0,3:T(8,128)(2,1)} fusion(f32[32,2,64,64]{2,3,1,0:T(8,128)} %fusion.50, bf16[32,64,2,1,64]{4,3,2,1,0:T(2,128)(2,1)} %get-tuple-element.20, f32[32,2,64,64]{2,3,1,0:T(8,128)} %get-tuple-element.23, f32[32,2,64]{2,1,0:T(2,128)S(1)} %get-tuple-element.22), kind=kOutput, calls=%fused_computation.29 | convolution fusion | flops 35655744 | bytes 3162112 | tf_op jit(solution)/shard_map/bhqk,bqhe->bkhe/dot_general | solution.py:116
  193.2 6.1 %fusion.26 = bf16[32,64,2,1,64]{1,4,2,0,3:T(8,128)(2,1)} fusion(f32[32,2,64,64]{2,3,1,0:T(8,128)} %fusion.50, bf16[32,64,2,1,64]{4,3,2,1,0:T(2,128)(2,1)} %get-tuple-element.21, f32[32,2,64,64]{2,3,1,0:T(8,128)} %get-tuple-element.23, f32[32,2,64]{2,1,0:T(2,128)S(1)} %get-tuple-element.22), kind=kOutput, calls=%fused_computation.30 | convolution fusion | flops 35655744 | bytes 3162112 | tf_op jit(solution)/shard_map/bhqk,bkhe->bqhe/dot_general | solution.py:113
  199.3 2.6 pad_maximum_fusion
  201.9 3.8 %copy.36 = bf16[32,64,2,3,64]{1,0,4,3,2:T(8,128)(2,1)} copy(bf16[32,64,2,3,64]{1,4,2,0,3:T(8,128)(2,1)S(1)} %pad_maximum_fusion) | data formatting | bytes 3145728 | tf_op jit(solution)/shard_map/stack | solution.py:119
  205.7 5.6 %reshape.129 = bf16[2048,384]{0,1:T(8,128)(2,1)} reshape(bf16[32,64,2,3,64]{1,0,4,3,2:T(8,128)(2,1)} %copy.36) | data formatting | bytes 3145728 | tf_op jit(solution)/shard_map/reshape | solution.py:119
  211.3 6.0 %convolution_convert_fusion = bf16[2048,1024]{1,0:T(8,128)(2,1)} fusion(bf16[2048,384]{0,1:T(8,128)(2,1)} %reshape.129, bf16[1024,384]{1,0:T(8,128)(2,1)} %bitcast.75), kind=kOutput, calls=%fused_computation.2 | convolution fusion | flops 1612709888 | bytes 6553600 | tf_op jit(solution)/shard_map/dot_general | solution.py:127
  220.9 2.9 convolution_convert_fusion.6
  224.7 7.0 %all-to-all-start.5 = ((bf16[16,128,64]{1,2,0:T(8,128)(2,1)}), bf16[16,128,64]{1,2,0:T(8,128)(2,1)S(1)}, u32[]{:S(2)}, u32[]{:S(2)}) async-start(bf16[16,128,64]{1,2,0:T(8,128)(2,1)} %bitcast.17), calls=%async_computation.6 | async-start | bytes 524288 | tf_op jit(solution)/shard_map/all_to_all | solution.py:38
  231.7 6.0 %convolution_convert_fusion.5 = bf16[1024,384]{1,0:T(8,128)(2,1)} fusion(bf16[2048,1024]{1,0:T(8,128)(2,1)} %bitcast, bf16[2048,384]{0,1:T(8,128)(2,1)} %reshape.129), kind=kOutput, calls=%fused_computation.26 | convolution fusion | flops 1611005952 | bytes 6553600 | tf_op jit(solution)/shard_map/dot_general | solution.py:122
  237.6 2.7 all-to-all-done.5
  240.4 4.5 %all-to-all-start.4 = ((bf16[16,64,384]{2,1,0:T(8,128)(2,1)}), bf16[16,64,384]{2,1,0:T(8,128)(2,1)S(1)}, u32[]{:S(2)}, u32[]{:S(2)}) async-start(bf16[16,64,384]{2,1,0:T(8,128)(2,1)} %bitcast.14), calls=%async_computation.5 | async-start | bytes 1572864 | tf_op jit(solution)/shard_map/all_to_all | solution.py:38
  245.8 14.1 %all-to-all-done.4 = bf16[16,64,384]{2,1,0:T(8,128)(2,1)S(1)} async-done(((bf16[16,64,384]{2,1,0:T(8,128)(2,1)}), bf16[16,64,384]{2,1,0:T(8,128)(2,1)S(1)}, u32[]{:S(2)}, u32[]{:S(2)}) %all-to-all-start.4) | async-done | bytes 786464 | tf_op jit(solution)/shard_map/all_to_all | solution.py:38
  260.6 58.4 %reduce-scatter.2.cloned.1.call-done = bf16[256,1024]{1,0:T(8,128)(2,1)} async-done(((bf16[2048,1024]{1,0:T(8,128)(2,1)}), bf16[256,1024]{1,0:T(8,128)(2,1)}) %reduce-scatter.2.cloned.1.call-update) | async-done | bytes 524304 | tf_op jit(solution)/shard_map/reduce_scatter | solution.py:126
  320.7 5.3 %all-reduce.4 = (f32[1024]{0:T(1024)S(1)}, f32[1024]{0:T(1024)S(1)}) all-reduce(f32[1024]{0:T(1024)S(1)} %get-tuple-element.5, f32[1024]{0:T(1024)S(1)} %get-tuple-element.8), channel_id=1, replica_groups=mesh['dp_0'=2,'dp_1'=4,'dp_2'=2,'tensor_0'=4,'tensor_1'=2] {'dp_0'}, use_global_device_ids=true, to_apply=%region_11.12 | all-reduce | flops 2048 | bytes 16384 | tf_op jit(solution)/shard_map/psum | solution.py:43
  326.0 8.5 %all-reduce.1 = (f32[1024]{0:T(1024)S(1)}, f32[1024]{0:T(1024)S(1)}) all-reduce(f32[1024]{0:T(1024)S(1)} %get-tuple-element.17, f32[1024]{0:T(1024)S(1)} %get-tuple-element.18), channel_id=1, replica_groups=mesh['dp_0'=2,'dp_1'=4,'dp_2'=2,'tensor_0'=4,'tensor_1'=2] {'dp_1'}, use_global_device_ids=true, to_apply=%region_12.13 | all-reduce | flops 2048 | bytes 16384 | tf_op jit(solution)/shard_map/psum | solution.py:43
  334.5 6.4 %all-reduce.3 = (f32[1024]{0:T(1024)S(1)}, f32[1024]{0:T(1024)S(1)}) all-reduce(f32[1024]{0:T(1024)S(1)} %get-tuple-element.11, f32[1024]{0:T(1024)S(1)} %get-tuple-element.12), channel_id=1, replica_groups=mesh['dp_0'=2,'dp_1'=4,'dp_2'=2,'tensor_0'=4,'tensor_1'=2] {'dp_2'}, use_global_device_ids=true, to_apply=%region_13.14 | all-reduce | flops 2048 | bytes 16384 | tf_op jit(solution)/shard_map/psum | solution.py:43
  340.9 7.4 %all-reduce = (f32[1024]{0:T(1024)S(1)}, f32[1024]{0:T(1024)S(1)}) all-reduce(f32[1024]{0:T(1024)S(1)} %get-tuple-element.15, f32[1024]{0:T(1024)S(1)} %get-tuple-element.16), channel_id=1, replica_groups=mesh['dp_0'=2,'dp_1'=4,'dp_2'=2,'tensor_0'=4,'tensor_1'=2] {'tensor_0'}, use_global_device_ids=true, to_apply=%region_14.15 | all-reduce | flops 2048 | bytes 16384 | tf_op jit(solution)/shard_map/psum | solution.py:43
  348.4 4.4 %all-reduce.2 = (f32[1024]{0:T(1024)}, f32[1024]{0:T(1024)}) all-reduce(f32[1024]{0:T(1024)S(1)} %get-tuple-element.9, f32[1024]{0:T(1024)S(1)} %get-tuple-element.10), channel_id=1, replica_groups=mesh['dp_0'=2,'dp_1'=4,'dp_2'=2,'tensor_0'=4,'tensor_1'=2] {'tensor_1'}, use_global_device_ids=true, to_apply=%region_15.16 | all-reduce | flops 2048 | bytes 16384 | tf_op jit(solution)/shard_map/psum | solution.py:43
  (46 shorter events, 20.5 us)
Async XLA Ops:
  7.2 36.9 %copy-start.3 = (bf16[256,1024]{1,0:T(8,128)(2,1)S(1)}, bf16[256,1024]{1,0:T(8,128)(2,1)}, u32[]{:S(2)}) copy-start(bf16[256,1024]{1,0:T(8,128)(2,1)} %param.8) | copy-start | bytes 1572868
  46.5 5.3 %copy-start.1 = (bf16[256,1024]{1,0:T(8,128)(2,1)S(1)}, bf16[256,1024]{1,0:T(8,128)(2,1)}, u32[]{:S(2)}) copy-start(bf16[256,1024]{1,0:T(8,128)(2,1)} %param.7) | copy-start | bytes 1572868
  46.5 5.7 %copy-start.4 = (f32[1024]{0:T(1024)S(1)}, f32[1024]{0:T(1024)}, u32[]{:S(2)}) copy-start(f32[1024]{0:T(1024)} %param.10) | copy-start | bytes 12292
  46.6 5.8 %copy-start.5 = (f32[1024]{0:T(1024)S(1)}, f32[1024]{0:T(1024)}, u32[]{:S(2)}) copy-start(f32[1024]{0:T(1024)} %param.11) | copy-start | bytes 12292
  46.6 53.9 %all-to-all-start.2 = ((bf16[8,256,1024]{2,1,0:T(8,128)(2,1)}), bf16[8,256,1024]{2,1,0:T(8,128)(2,1)}, u32[]{:S(2)}, u32[]{:S(2)}) async-start(bf16[8,256,1024]{2,1,0:T(8,128)(2,1)} %broadcast_in_dim.24), calls=%async_computation.2 | async-start | bytes 8388608 | tf_op jit(solution)/shard_map/all_to_all | solution.py:24
  103.0 4.8 %copy-start.6 = (s32[32]{0:T(128)S(1)}, s32[32]{0:T(128)}, u32[]{:S(2)}) copy-start(s32[32]{0:T(128)} %param.9) | copy-start | bytes 388
  103.0 52.3 %all-to-all-start = ((bf16[8,256,1024]{2,1,0:T(8,128)(2,1)}), bf16[8,256,1024]{2,1,0:T(8,128)(2,1)}, u32[]{:S(2)}, u32[]{:S(2)}) async-start(bf16[8,256,1024]{2,1,0:T(8,128)(2,1)} %broadcast_in_dim.16), calls=%async_computation | async-start | bytes 8388608 | tf_op jit(solution)/shard_map/all_to_all | solution.py:24
  107.6 211.4 %reduce-scatter.2.cloned.1.call-start = ((), (), s32[]{:S(2)}) async-start(), calls=%async_computation.7 | async-start | bytes 4718592 | tf_op jit(solution)/shard_map/reduce_scatter | solution.py:126
  110.6 2.0 copy-start
  164.8 12.1 %copy-start.2 = (bf16[32,64,2,64]{1,3,2,0:T(8,128)(2,1)S(1)}, bf16[32,64,2,64]{1,3,2,0:T(8,128)(2,1)}, u32[]{:S(2)}) copy-start(bf16[32,64,2,64]{1,3,2,0:T(8,128)(2,1)} %copy.34) | copy-start | bytes 1572868
  224.7 15.7 %all-to-all-start.5 = ((bf16[16,128,64]{1,2,0:T(8,128)(2,1)}), bf16[16,128,64]{1,2,0:T(8,128)(2,1)S(1)}, u32[]{:S(2)}, u32[]{:S(2)}) async-start(bf16[16,128,64]{1,2,0:T(8,128)(2,1)} %bitcast.17), calls=%async_computation.6 | async-start | bytes 524288 | tf_op jit(solution)/shard_map/all_to_all | solution.py:38
  240.4 19.5 %all-to-all-start.4 = ((bf16[16,64,384]{2,1,0:T(8,128)(2,1)}), bf16[16,64,384]{2,1,0:T(8,128)(2,1)S(1)}, u32[]{:S(2)}, u32[]{:S(2)}) async-start(bf16[16,64,384]{2,1,0:T(8,128)(2,1)} %bitcast.14), calls=%async_computation.5 | async-start | bytes 1572864 | tf_op jit(solution)/shard_map/all_to_all | solution.py:38
Sparse Core Ops, SparseCore 0:
  217.4 101.5 reduce-scatter.1
where the time goes:
time: 365 us; the launch traced here: 362 us
  waiting for transfers between devices  162 us (44%)
  blocking collectives  67.3 us (18%)
  matrix products  45.3 us (12%)
  local copies, waits for them, and re-layouts  40.3 us (11%)
  starting transfers between devices  21.5 us (6%)
  between operations  14.2 us (4%)
  other arithmetic  11.4 us (3%)
    all_to_all x2, waiting for transfers between devices, sent_to_all(): return lax.all_to_all(copies, axis, split_axis=0, concat_axis=0, tiled=True)  86.7 us
    reduce_scatter x1, waiting for transfers between devices, on_device(): lax.psum_scatter(lax.dot_general(grad_proj, qkv_cols, (((1,), (1,)), ((),...  58.4 us
    all_to_all x2, blocking collectives, sent_to_all(): return lax.all_to_all(copies, axis, split_axis=0, concat_axis=0, tiled=True)  35.2 us
    psum x5, blocking collectives, by_axis(): return functools.reduce(lax.psum, axes, value)  32.1 us
    all_to_all x2, waiting for transfers between devices, summed_on_arrival(): lax.all_to_all(pieces, axis, split_axis=0, concat_axis=0, tiled=True)  16.8 us
    slice x1, local copies, waits for them, and re-layouts, on_device(): value_rows = projected[:, :, :, 2]  12.1 us
    all_to_all x2, starting transfers between devices, summed_on_arrival(): lax.all_to_all(pieces, axis, split_axis=0, concat_axis=0, tiled=True)  11.5 us
    all_to_all x2, starting transfers between devices, sent_to_all(): return lax.all_to_all(copies, axis, split_axis=0, concat_axis=0, tiled=True)  9.95 us
  transfers between devices with their start and end apart: 5, of which 5 were waited for; matrix products, arithmetic and copies ran while one was open for 6% of the time, Pallas kernels for 0%

commit v1 on v0

v1 whole, which is shorter than its diff:
```python
import functools

import jax
import jax.numpy as jnp
from jax import lax
from jax.experimental import pallas as pl
from jax.experimental.pallas import tpu as pltpu
from jax.sharding import Mesh
from jax.sharding import PartitionSpec as P

D = 1024
HEAD = 64
CAP = 64
TENSOR = ("tensor_0", "tensor_1")
DP = ("dp_0", "dp_1", "dp_2")
DP_TENSOR = ("dp_0", "dp_1", "dp_2", "tensor_0", "tensor_1")
MESH = pl.DeviceIdType.MESH
F32 = jnp.float32
BF16 = jnp.bfloat16

ROWS = (48, 48, 48, 48, 32, 32)
FIRST = (0, 48, 96, 144, 192, 224)
COLOURS = 6
BITS = 6
BASE = ("x0", "y0", "z0", "x1", "y1", "z1")


def order(colour):
    return [BASE[(colour + s) % BITS] for s in range(BITS)]


def gray(x, y, z):
    return {
        "x0": ((x + 1) // 2) % 2,
        "x1": x // 2,
        "y0": ((y + 1) // 2) % 2,
        "y1": y // 2,
        "z0": ((z + 1) // 2) % 2,
        "z1": z // 2,
    }


def bits_of(place, colour):
    return [place[name] for name in order(colour)]


def joined(bits):
    total = 0
    for s, bit in enumerate(bits):
        total = total + bit * (1 << s)
    return total


def held(bits, p):
    if p == 0:
        return joined(bits), 1
    own = [0] * (p - 1) + [1 - bits[p - 1]] + list(bits[p:])
    return joined(own), 1 << (p - 1)


def across(bits, s):
    return list(bits[:s]) + [1 - bits[s]] + list(bits[s + 1 :])


PIECE_AT = []
_at = 0
for _p in range(BITS):
    PIECE_AT.append(_at)
    _at += (BITS - _p) * max(1, (1 << _p) // 2)
BLOCKS = 1 << BITS


def dot(a, b, dims):
    return lax.dot_general(a, b, (dims, ((), ())), preferred_element_type=F32)


def kernel(
    tok_ref,
    up_ref,
    counts_ref,
    gain_ref,
    bias_ref,
    wq_ref,
    wo_ref,
    dtok_ref,
    dq_ref,
    do_ref,
    dgain_ref,
    dbias_ref,
    *scratch,
):
    w_bufs = scratch[0:6]
    g_bufs = scratch[6:12]
    q_bufs = scratch[12:18]
    (
        mine,
        theirs,
        x_ref,
        u_ref,
        live_ref,
        xhat_ref,
        rstd_ref,
        wt_ref,
        wot_ref,
        proj_ref,
        gatt_ref,
        att_ref,
        gproj_ref,
        gn_own,
        gn_out,
        gn_in,
        sum_ref,
        sum_in,
        last_own,
        last_in,
        ag_send,
        ag_recv,
        rs_send,
        rs_recv,
        pair_send,
        pair_recv,
        sum_send,
        sum_recv,
    ) = scratch[18:]

    yh, x, c = (lax.axis_index(name) for name in DP)
    z, yl = (lax.axis_index(name) for name in TENSOR)
    y = 2 * yh + yl
    place = gray(x, y, z)
    peer = {
        "x0": {"dp_1": x + 1 - 2 * (x % 2)},
        "x1": {"dp_1": 3 - x},
        "y0": {"tensor_1": 1 - yl},
        "y1": {"dp_0": 1 - yh, "tensor_1": 1 - yl},
        "z0": {"tensor_0": z + 1 - 2 * (z % 2)},
        "z1": {"tensor_0": 3 - z},
        "c": {"dp_2": 1 - c},
    }
    bits = [bits_of(place, k) for k in range(COLOURS)]

    barrier = pltpu.get_barrier_semaphore()
    for name in peer:
        pl.semaphore_signal(barrier, inc=1, device_id=peer[name], device_id_type=MESH)

    def remote(src, dst, send, recv, name):
        return pltpu.make_async_remote_copy(
            src_ref=src,
            dst_ref=dst,
            send_sem=send,
            recv_sem=recv,
            device_id=peer[name],
            device_id_type=MESH,
        )

    def pair_copy(i, src, dst):
        return remote(src, dst, pair_send.at[i], pair_recv.at[i], "c")

    wq_t = wq_ref[...].astype(F32).T
    wo_f = wo_ref[...].astype(F32)
    for h in range(2):
        part = jnp.concatenate(
            [wq_t[192 * h : 192 * (h + 1)], wo_f[64 * h : 64 * (h + 1)]], axis=0
        )
        mine[h] = jnp.concatenate([part, part], axis=1).astype(BF16)

    pl.semaphore_wait(barrier, len(peer))
    first = pair_copy(0, mine.at[1 - c], theirs)
    first.start()
    first.wait()
    lane = lax.broadcasted_iota(jnp.int32, (256, 128), 1)
    own_half = (lane < 64) == (c == 0)
    block = jnp.where(own_half, mine[c].astype(F32), theirs[...].astype(F32)).astype(BF16)
    for k in range(COLOURS):
        w_bufs[k][joined(bits[k])] = block[FIRST[k] : FIRST[k] + ROWS[k]]

    def ag_copy(k, s, p):
        at, n = held(bits[k], p)
        part = w_bufs[k].at[pl.ds(at, n)]
        return remote(part, part, ag_send.at[k], ag_recv.at[k, s], order(k)[s])

    def ag_sends(p):
        for k in range(COLOURS):
            if p > 0:
                at, n = held(bits[k], p)
                part = w_bufs[k].at[pl.ds(at, n)]
                pltpu.make_async_copy(part, part, ag_recv.at[k, p - 1]).wait()
            if p < BITS:
                ag_copy(k, p, p).start()
        for s in range(p + 1, BITS):
            for k in range(COLOURS):
                ag_copy(k, s, p).start()

    ag_sends(0)

    values = tok_ref[...].astype(F32)
    centre = jnp.mean(values, axis=-1, keepdims=True)
    shifted = values - centre
    variance = jnp.mean(shifted * shifted, axis=-1, keepdims=True)
    inverse = lax.rsqrt(variance + 1e-6)
    scaled = shifted * inverse
    xhat_ref[...] = scaled
    rstd_ref[...] = jnp.broadcast_to(inverse, (256, 128))
    own_rows = pl.ds(pl.multiple_of(c * 256, 256), 256)
    x_ref[own_rows, :] = (scaled * gain_ref[...] + bias_ref[...]).astype(BF16)
    start = (2 * z + yl) * 4
    row = lax.broadcasted_iota(jnp.int32, (256, 128), 0)
    image = row // CAP
    count = jnp.where(
        image < 2,
        jnp.where(image == 0, counts_ref[start], counts_ref[start + 1]),
        jnp.where(image == 2, counts_ref[start + 2], counts_ref[start + 3]),
    )
    live = jnp.where(row % CAP < count, 1.0, 0.0).astype(F32)
    live_ref[own_rows, :] = live
    u_ref[own_rows, :] = (up_ref[...].astype(F32) * live[:, :1]).astype(BF16)
    shared = [
        pair_copy(1, x_ref.at[own_rows], x_ref.at[own_rows]),
        pair_copy(2, u_ref.at[own_rows], u_ref.at[own_rows]),
        pair_copy(3, live_ref.at[own_rows], live_ref.at[own_rows]),
    ]
    for copy in shared:
        copy.start()

    for p in range(1, BITS + 1):
        ag_sends(p)

    def block_at(k, zz, yy, xx):
        return joined(bits_of(gray(xx, yy, zz), k))

    @pl.loop(0, 4)
    def _(zz):
        for yy in range(4):
            t_rows = pl.multiple_of((2 * zz + yy % 2) * 192, 192)
            o_rows = pl.multiple_of((2 * zz + yy % 2) * 64, 64)
            for xx in range(4):
                at = ((yy // 2) * 4 + xx) * 128
                for k in range(4):
                    wt_ref[pl.ds(t_rows + FIRST[k], 48), at : at + 128] = w_bufs[k][
                        block_at(k, zz, yy, xx)
                    ]
                for k in range(4, 6):
                    wot_ref[pl.ds(o_rows + FIRST[k] - 192, 32), at : at + 128] = w_bufs[k][
                        block_at(k, zz, yy, xx)
                    ]

    for copy in shared:
        copy.wait()

    @pl.loop(0, 4)
    def _(i):
        rows = pl.ds(pl.multiple_of(i * 384, 384), 384)
        proj_ref[rows, :] = dot(wt_ref[rows, :], x_ref[...], ((1,), (1,))).astype(BF16)

    @pl.loop(0, 2)
    def _(i):
        rows = pl.ds(pl.multiple_of(i * 256, 256), 256)
        gatt_ref[rows, :] = dot(wot_ref[rows, :], u_ref[...], ((1,), (1,))).astype(BF16)

    left = lax.broadcasted_iota(jnp.int32, (64, 128), 1) < 64

    def folded(a):
        return jnp.where(left, a[:64], a[64:])

    def unfolded(a):
        zero = jnp.zeros_like(a)
        return jnp.concatenate([jnp.where(left, a, zero), jnp.where(left, zero, a)], axis=0).astype(
            BF16
        )

    @pl.loop(0, 8)
    def _(t):
        base = pl.multiple_of(t * 192, 192)
        o_base = pl.multiple_of(t * 64, 64)
        for pair in range(4):
            lanes = slice(pair * 128, pair * 128 + 128)
            q = proj_ref[pl.ds(base, 64), lanes]
            k = proj_ref[pl.ds(base + 64, 64), lanes]
            v = proj_ref[pl.ds(base + 128, 64), lanes]
            g = gatt_ref[pl.ds(o_base, 64), lanes]
            key_live = folded(live_ref[lanes, :]) > 0.5
            scores = folded(dot(k, q, ((0,), (0,)))) * 0.125
            scores = jnp.where(key_live, scores, -1e30)
            top = jnp.max(scores, axis=0, keepdims=True)
            powers = jnp.exp(scores - top)
            probs = powers / jnp.sum(powers, axis=0, keepdims=True)
            grad_probs = folded(dot(v, g, ((0,), (0,))))
            delta = jnp.sum(probs * grad_probs, axis=0, keepdims=True)
            grad_scores = unfolded(probs * (grad_probs - delta) * 0.125)
            probs_low = unfolded(probs)
            att_ref[pl.ds(o_base, 64), lanes] = dot(v, probs_low, ((1,), (0,))).astype(BF16)
            gproj_ref[pl.ds(base, 64), lanes] = dot(k, grad_scores, ((1,), (0,))).astype(BF16)
            gproj_ref[pl.ds(base + 64, 64), lanes] = dot(q, grad_scores, ((1,), (1,))).astype(BF16)
            gproj_ref[pl.ds(base + 128, 64), lanes] = dot(g, probs_low, ((1,), (1,))).astype(BF16)

    @pl.loop(0, 4)
    def _(zz):
        o_rows = pl.ds(pl.multiple_of(zz * 128, 128), 128)
        t_rows = pl.ds(pl.multiple_of(zz * 384, 384), 384)
        out = dot(att_ref[o_rows, :], u_ref[...], ((1,), (0,))).astype(BF16)
        for yy in range(4):
            for xx in range(4):
                at = ((yy // 2) * 4 + xx) * 128
                for k in range(4, 6):
                    low = (yy % 2) * 64 + FIRST[k] - 192
                    g_bufs[k][block_at(k, zz, yy, xx)] = out[low : low + 32, at : at + 128]
        out = dot(gproj_ref[t_rows, :], x_ref[...], ((1,), (0,))).astype(BF16)
        for yy in range(4):
            for xx in range(4):
                at = ((yy // 2) * 4 + xx) * 128
                for k in range(4):
                    low = (yy % 2) * 192 + FIRST[k]
                    g_bufs[k][block_at(k, zz, yy, xx)] = out[low : low + 48, at : at + 128]

    def q_part(k, p, s, count):
        n = max(1, (1 << p) // 2)
        return q_bufs[k].at[pl.ds(PIECE_AT[p] + (s - p) * n, count * n)]

    def rs_sends(s):
        for p in range(s, -1, -1):
            for k in range(COLOURS):
                at, n = held(across(bits[k], s), p)
                remote(
                    g_bufs[k].at[pl.ds(at, n)],
                    q_part(k, p, s, 1),
                    rs_send.at[k],
                    rs_recv.at[k, p],
                    order(k)[s],
                ).start()

    rs_sends(BITS - 1)

    for other in range(2):
        for half in range(2):
            rows = pl.ds(
                pl.multiple_of((c if other == 0 else 1 - c) * 256 + half * 128, 128), 128
            )
            part = dot(gproj_ref[:, rows], wt_ref[...], ((0,), (0,)))
            if other == 0:
                gn_own[half * 128 : half * 128 + 128] = part
            else:
                gn_out[half * 128 : half * 128 + 128] = part.astype(BF16)
    swap = pair_copy(4, gn_out, gn_in)
    swap.start()

    def sum_step(i, name):
        return remote(sum_ref.at[i], sum_in.at[i], sum_send.at[i], sum_recv.at[i], name)

    def sum_finish(i, name):
        sum_step(i, name).wait_recv()
        sum_ref[i + 1] = sum_ref[i] + sum_in[i]

    names = ("c",) + BASE
    for s in range(BITS - 2, -1, -1):
        p = s + 1
        for k in range(COLOURS):
            at, n = held(bits[k], p)
            count = BITS - p
            whole = q_part(k, p, p, count)
            pltpu.make_async_copy(whole, whole, rs_recv.at[k, p]).wait()

            def add(i, _, k=k, p=p, n=n, at=at, count=count):
                total = g_bufs[k][at + i].astype(F32)
                for j in range(count):
                    total = total + q_bufs[k][PIECE_AT[p] + j * n + i].astype(F32)
                g_bufs[k][at + i] = total.astype(BF16)
                return 0

            lax.fori_loop(0, n, add, 0)
        rs_sends(s)
        if s == BITS - 2:
            swap.wait()
            live_own = live_ref[own_rows, :][:, :1]
            scaled = xhat_ref[...]
            grad_normed = gn_own[...] + gn_in[...].astype(F32)
            sum_ref[0] = jnp.concatenate(
                [
                    jnp.sum(grad_normed * scaled, axis=0, keepdims=True),
                    jnp.sum(grad_normed, axis=0, keepdims=True),
                ],
                axis=0,
            )
            sum_step(0, names[0]).start()
            g = grad_normed * gain_ref[...]
            grad_ln = rstd_ref[...][:, :1] * (
                g
                - jnp.mean(g, axis=-1, keepdims=True)
                - scaled * jnp.mean(g * scaled, axis=-1, keepdims=True)
            )
            dtok_ref[...] = (up_ref[...].astype(F32) * live_own + grad_ln).astype(BF16)
        else:
            i = BITS - 3 - s
            sum_finish(i, names[i])
            sum_step(i + 1, names[i + 1]).start()
    for k in range(COLOURS):
        whole = q_part(k, 0, 0, BITS)
        pltpu.make_async_copy(whole, whole, rs_recv.at[k, 0]).wait()
        total = g_bufs[k][joined(bits[k])].astype(F32)
        for s in range(BITS):
            total = total + q_bufs[k][s].astype(F32)
        last_own[FIRST[k] : FIRST[k] + ROWS[k]] = total
    final = pair_copy(5, last_own, last_in)
    final.start()
    for i in range(BITS - 2, 7):
        sum_finish(i, names[i])
        if i < 6:
            sum_step(i + 1, names[i + 1]).start()
        if i == BITS - 2:
            final.wait()
            for h in range(2):
                blk = jnp.where(c == h, last_own[...], last_in[...])
                blk = jnp.where(c == 0, blk, pltpu.roll(blk, 64, 1))[:, :64]
                dq_ref[:, 192 * h : 192 * (h + 1)] = blk[:192].T
                do_ref[64 * h : 64 * (h + 1), :] = blk[192:]
    dgain_ref[...] = sum_ref[7, 0:1]
    dbias_ref[...] = sum_ref[7, 1:2]
    for i in range(7):
        sum_step(i, names[i]).wait_send()
    for k in range(COLOURS):
        for bufs, sems in ((w_bufs, ag_send), (g_bufs, rs_send)):
            part = bufs[k].at[pl.ds(0, BLOCKS - 1)]
            pltpu.make_async_copy(part, part, sems.at[k]).wait()


def on_device(tokens, upstream, counts, norm_gain, norm_bias, w_qkv, w_out):
    vmem = pl.BlockSpec(memory_space=pltpu.VMEM)
    blocks = [pltpu.VMEM((BLOCKS, r, 128), BF16) for r in ROWS]
    parts = [pltpu.VMEM((BLOCKS - 1, r, 128), BF16) for r in ROWS]
    dma = pltpu.SemaphoreType.DMA
    outs = pl.pallas_call(
        kernel,
        out_shape=(
            jax.ShapeDtypeStruct((256, D), BF16),
            jax.ShapeDtypeStruct((64, 384), F32),
            jax.ShapeDtypeStruct((128, 64), F32),
            jax.ShapeDtypeStruct((1, D), F32),
            jax.ShapeDtypeStruct((1, D), F32),
        ),
        in_specs=[vmem, vmem, pl.BlockSpec(memory_space=pltpu.SMEM)] + [vmem] * 4,
        out_specs=(vmem,) * 5,
        scratch_shapes=[
            *blocks,
            *blocks,
            *parts,
            pltpu.VMEM((2, 256, 128), BF16),
            pltpu.VMEM((256, 128), BF16),
            pltpu.VMEM((512, D), BF16),
            pltpu.VMEM((512, D), BF16),
            pltpu.VMEM((512, 128), F32),
            pltpu.VMEM((256, D), F32),
            pltpu.VMEM((256, 128), F32),
            pltpu.VMEM((1536, D), BF16),
            pltpu.VMEM((512, D), BF16),
            pltpu.VMEM((1536, 512), BF16),
            pltpu.VMEM((512, 512), BF16),
            pltpu.VMEM((512, 512), BF16),
            pltpu.VMEM((1536, 512), BF16),
            pltpu.VMEM((256, D), F32),
            pltpu.VMEM((256, D), BF16),
            pltpu.VMEM((256, D), BF16),
            pltpu.VMEM((8, 2, D), F32),
            pltpu.VMEM((7, 2, D), F32),
            pltpu.VMEM((256, 128), F32),
            pltpu.VMEM((256, 128), F32),
            dma((COLOURS,)),
            dma((COLOURS, BITS)),
            dma((COLOURS,)),
            dma((COLOURS, BITS)),
            dma((6,)),
            dma((6,)),
            dma((7,)),
            dma((7,)),
        ],
        compiler_params=pltpu.CompilerParams(
            collective_id=0, has_side_effects=True, vmem_limit_bytes=60 * 1024 * 1024
        ),
    )(
        tokens,
        upstream,
        counts,
        norm_gain.reshape(1, D),
        norm_bias.reshape(1, D),
        w_qkv,
        w_out,
    )
    dtok, dq, do, dgain, dbias = outs
    return dtok, dq, do, dgain.reshape(D), dbias.reshape(D)


def solution(mesh):
    finer = Mesh(
        mesh.devices.reshape(2, 4, 2, 4, 2), ("dp_0", "dp_1", "dp_2", "tensor_0", "tensor_1")
    )
    in_specs = (
        P(DP_TENSOR, None),
        P(DP_TENSOR, None),
        P(DP),
        P(),
        P(),
        P(DP, TENSOR),
        P(TENSOR, DP),
    )
    out_specs = (P(DP_TENSOR, None), P(DP, TENSOR), P(TENSOR, DP), P(), P())
    return jax.shard_map(
        on_device, mesh=finer, in_specs=in_specs, out_specs=out_specs, check_vma=False
    )
```

time: 365 us -> 92.3 us (0.25)
  the two profiles are of different devices: /device:TPU:1 before, /device:TPU:0 now
where the time goes in v1:
time: 92.3 us; the launch traced here: 91.9 us
  Pallas kernels  84.5 us (92%)
  local copies, waits for them, and re-layouts  6.81 us (7%)
    pallas_call x1, Pallas kernels, on_device(): pl.pallas_call(kernel, out_shape=(jax.ShapeDtypeStruct((256, D), BF16), j...  84.5 us
    unnamed x12, local copies, waits for them, and re-layouts  6.81 us

profile of v1, /device:TPU:0, one launch (start us, length us, event | category | flops | bytes accessed | tf_op | source)
XLA Modules:
  0.0 91.9 jit_solution(3905896754959009166)
XLA Ops:
  0.6 1.4 %copy.12.wo_ref = bf16[128,64]{1,0:T(8,128)(2,1)} copy(bf16[128,64]{0,1:T(8,128)(2,1)} %param.13) | data formatting | bytes 32768 | tf_op args[6]
  2.1 84.5 %shard_map.110 = (bf16[256,1024]{1,0:T(8,128)(2,1)}, f32[64,384]{1,0:T(8,128)}, f32[128,64]{1,0:T(8,128)}, f32[1,1024]{1,0:T(1,128)}, f32[1,1024]{1,0:T(1,128)}) custom-call(bf16[256,1024]{1,0:T(8,128)(2,1)} %tok_ref.1, bf16[256,1024]{1,0:T(8,128)(2,1)} %up_ref.1, s32[32]{0:T(128)} %counts_ref.1, f32[1,1024]{1,0:T(1,128)} %bitcast.4, f32[1,1024]{1,0:T(1,128)} %bitcast.5, ...), custom_call_target="tpu_custom_call" | custom-call | tf_op jit(solution)/shard_map/pallas_call | solution.py:429
  86.6 1.5 %copy.13 = f32[128,64]{0,1:T(8,128)} copy(f32[128,64]{1,0:T(8,128)} %get-tuple-element.17) | data formatting | bytes 65536
  88.1 0.0 copy-start
  88.1 1.9 %copy.18 = bf16[256,1024]{1,0:T(8,128)(2,1)} copy(bf16[256,1024]{1,0:T(8,128)(2,1)} %get-tuple-element.25) | data formatting | bytes 1048576
  90.0 0.0 copy-done
  90.0 0.0 copy-start.2
  90.0 0.6 copy.19
  90.7 0.0 copy-done.2
  90.7 0.0 copy-start.1
  90.7 0.6 copy.20
  91.3 0.1 copy-done.1
  91.4 0.6 copy.21
Async XLA Ops:
  88.1 1.9 %copy-start = (f32[64,384]{1,0:T(8,128)S(1)}, f32[64,384]{1,0:T(8,128)}, u32[]{:S(2)}) copy-start(f32[64,384]{1,0:T(8,128)} %get-tuple-element.26) | copy-start | bytes 294916
  90.0 0.7 copy-start.2
  90.7 0.7 copy-start.1

commit v2 on v1

--- a/solution.py
+++ b/solution.py
@@ -75,18 +75,16 @@
 
 
 def kernel(
-    tok_ref,
-    up_ref,
-    counts_ref,
-    gain_ref,
-    bias_ref,
-    wq_ref,
-    wo_ref,
-    dtok_ref,
-    dq_ref,
-    do_ref,
-    dgain_ref,
-    dbias_ref,
+    tok_in,
+    up_in,
+    counts_in,
+    gain_in,
+    bias_in,
+    wq_in,
+    wo_in,
+    dtok_out,
+    last_ref,
+    sums_ref,
     *scratch,
 ):
     w_bufs = scratch[0:6]
@@ -115,13 +113,34 @@
         last_in,
         ag_send,
         ag_recv,
-        rs_send,
+        rs_send_sem,
         rs_recv,
         pair_send,
         pair_recv,
         sum_send,
         sum_recv,
+        tok_ref,
+        up_ref,
+        wq_ref,
+        wo_ref,
+        gain_ref,
+        bias_ref,
+        counts_ref,
+        dtok_ref,
+        load_sem,
     ) = scratch[18:]
+
+    loads = [
+        pltpu.make_async_copy(wq_in, wq_ref, load_sem.at[0]),
+        pltpu.make_async_copy(wo_in, wo_ref, load_sem.at[1]),
+        pltpu.make_async_copy(tok_in, tok_ref, load_sem.at[2]),
+        pltpu.make_async_copy(up_in, up_ref, load_sem.at[3]),
+        pltpu.make_async_copy(gain_in, gain_ref, load_sem.at[4]),
+        pltpu.make_async_copy(bias_in, bias_ref, load_sem.at[5]),
+        pltpu.make_async_copy(counts_in, counts_ref, load_sem.at[6]),
+    ]
+    for load in loads:
+        load.start()
 
     yh, x, c = (lax.axis_index(name) for name in DP)
     z, yl = (lax.axis_index(name) for name in TENSOR)
@@ -155,8 +174,10 @@
     def pair_copy(i, src, dst):
         return remote(src, dst, pair_send.at[i], pair_recv.at[i], "c")
 
+    loads[0].wait()
+    loads[1].wait()
     wq_t = wq_ref[...].astype(F32).T
-    wo_f = wo_ref[...].astype(F32)
+    wo_f = wo_ref[...].astype(F32).T
     for h in range(2):
         part = jnp.concatenate(
             [wq_t[192 * h : 192 * (h + 1)], wo_f[64 * h : 64 * (h + 1)]], axis=0
@@ -192,6 +213,8 @@
 
     ag_sends(0)
 
+    for load in loads[2:]:
+        load.wait()
     values = tok_ref[...].astype(F32)
     centre = jnp.mean(values, axis=-1, keepdims=True)
     shifted = values - centre
@@ -292,6 +315,20 @@
             gproj_ref[pl.ds(base + 64, 64), lanes] = dot(q, grad_scores, ((1,), (1,))).astype(BF16)
             gproj_ref[pl.ds(base + 128, 64), lanes] = dot(g, probs_low, ((1,), (1,))).astype(BF16)
 
+    swap = pair_copy(4, gn_out, gn_in)
+    for other in (1, 0):
+        for half in range(2):
+            rows = pl.ds(
+                pl.multiple_of((c if other == 0 else 1 - c) * 256 + half * 128, 128), 128
+            )
+            part = dot(gproj_ref[:, rows], wt_ref[...], ((0,), (0,)))
+            if other == 0:
+                gn_own[half * 128 : half * 128 + 128] = part
+            else:
+                gn_out[half * 128 : half * 128 + 128] = part.astype(BF16)
+        if other == 1:
+            swap.start()
+
     @pl.loop(0, 4)
     def _(zz):
         o_rows = pl.ds(pl.multiple_of(zz * 128, 128), 128)
@@ -315,82 +352,76 @@
         n = max(1, (1 << p) // 2)
         return q_bufs[k].at[pl.ds(PIECE_AT[p] + (s - p) * n, count * n)]
 
-    def rs_sends(s):
-        for p in range(s, -1, -1):
+    def rs_send(k, s, p):
+        at, n = held(across(bits[k], s), p)
+        remote(
+            g_bufs[k].at[pl.ds(at, n)],
+            q_part(k, p, s, 1),
+            rs_send_sem.at[k],
+            rs_recv.at[k, p],
+            order(k)[s],
+        ).start()
+
+    def rs_rest(s):
+        for p in range(s - 1, -1, -1):
             for k in range(COLOURS):
-                at, n = held(across(bits[k], s), p)
-                remote(
-                    g_bufs[k].at[pl.ds(at, n)],
-                    q_part(k, p, s, 1),
-                    rs_send.at[k],
-                    rs_recv.at[k, p],
-                    order(k)[s],
-                ).start()
-
-    rs_sends(BITS - 1)
-
-    for other in range(2):
-        for half in range(2):
-            rows = pl.ds(
-                pl.multiple_of((c if other == 0 else 1 - c) * 256 + half * 128, 128), 128
-            )
-            part = dot(gproj_ref[:, rows], wt_ref[...], ((0,), (0,)))
-            if other == 0:
-                gn_own[half * 128 : half * 128 + 128] = part
-            else:
-                gn_out[half * 128 : half * 128 + 128] = part.astype(BF16)
-    swap = pair_copy(4, gn_out, gn_in)
-    swap.start()
-
-    def sum_step(i, name):
-        return remote(sum_ref.at[i], sum_in.at[i], sum_send.at[i], sum_recv.at[i], name)
-
-    def sum_finish(i, name):
-        sum_step(i, name).wait_recv()
+                rs_send(k, s, p)
+
+    names = tuple(order(0)[::-1]) + ("c",)
+
+    def sum_step(i):
+        return remote(sum_ref.at[i], sum_in.at[i], sum_send.at[i], sum_recv.at[i], names[i])
+
+    def sum_finish(i):
+        sum_step(i).wait_recv()
         sum_ref[i + 1] = sum_ref[i] + sum_in[i]
 
-    names = ("c",) + BASE
+    swap.wait()
+    scaled = xhat_ref[...]
+    grad_normed = gn_own[...] + gn_in[...].astype(F32)
+    gn_own[...] = grad_normed
+    sum_ref[0] = jnp.concatenate(
+        [
+            jnp.sum(grad_normed * scaled, axis=0, keepdims=True),
+            jnp.sum(grad_normed, axis=0, keepdims=True),
+        ],
+        axis=0,
+    )
+    sum_step(0).start()
+    for k in range(COLOURS):
+        rs_send(k, BITS - 1, BITS - 1)
+    rs_rest(BITS - 1)
+
+    live_own = live_ref[own_rows, :][:, :1]
+    scaled = xhat_ref[...]
+    g = gn_own[...] * gain_ref[...]
+    grad_ln = rstd_ref[...][:, :1] * (
+        g
+        - jnp.mean(g, axis=-1, keepdims=True)
+        - scaled * jnp.mean(g * scaled, axis=-1, keepdims=True)
+    )
+    dtok_ref[...] = (up_ref[...].astype(F32) * live_own + grad_ln).astype(BF16)
+    store = pltpu.make_async_copy(dtok_ref, dtok_out, load_sem.at[7])
+    store.start()
+
     for s in range(BITS - 2, -1, -1):
         p = s + 1
+        count = BITS - p
         for k in range(COLOURS):
             at, n = held(bits[k], p)
-            count = BITS - p
             whole = q_part(k, p, p, count)
             pltpu.make_async_copy(whole, whole, rs_recv.at[k, p]).wait()
-
-            def add(i, _, k=k, p=p, n=n, at=at, count=count):
-                total = g_bufs[k][at + i].astype(F32)
-                for j in range(count):
-                    total = total + q_bufs[k][PIECE_AT[p] + j * n + i].astype(F32)
-                g_bufs[k][at + i] = total.astype(BF16)
-                return 0
-
-            lax.fori_loop(0, n, add, 0)
-        rs_sends(s)
-        if s == BITS - 2:
-            swap.wait()
-            live_own = live_ref[own_rows, :][:, :1]
-            scaled = xhat_ref[...]
-            grad_normed = gn_own[...] + gn_in[...].astype(F32)
-            sum_ref[0] = jnp.concatenate(
-                [
-                    jnp.sum(grad_normed * scaled, axis=0, keepdims=True),
-                    jnp.sum(grad_normed, axis=0, keepdims=True),
-                ],
-                axis=0,
-            )
-            sum_step(0, names[0]).start()
-            g = grad_normed * gain_ref[...]
-            grad_ln = rstd_ref[...][:, :1] * (
-                g
-                - jnp.mean(g, axis=-1, keepdims=True)
-                - scaled * jnp.mean(g * scaled, axis=-1, keepdims=True)
-            )
-            dtok_ref[...] = (up_ref[...].astype(F32) * live_own + grad_ln).astype(BF16)
-        else:
-            i = BITS - 3 - s
-            sum_finish(i, names[i])
-            sum_step(i + 1, names[i + 1]).start()
+            total = g_bufs[k][pl.ds(at, n)].astype(F32)
+            for j in range(count):
+                first_at = PIECE_AT[p] + j * n
+                total = total + q_bufs[k][first_at : first_at + n].astype(F32)
+            g_bufs[k][pl.ds(at, n)] = total.astype(BF16)
+            if k == 0:
+                i = BITS - 2 - s
+                sum_finish(i)
+                sum_step(i + 1).start()
+            rs_send(k, s, s)
+        rs_rest(s)
     for k in range(COLOURS):
         whole = q_part(k, 0, 0, BITS)
         pltpu.make_async_copy(whole, whole, rs_recv.at[k, 0]).wait()
@@ -400,43 +431,48 @@
         last_own[FIRST[k] : FIRST[k] + ROWS[k]] = total
     final = pair_copy(5, last_own, last_in)
     final.start()
-    for i in range(BITS - 2, 7):
-        sum_finish(i, names[i])
-        if i < 6:
-            sum_step(i + 1, names[i + 1]).start()
-        if i == BITS - 2:
-            final.wait()
-            for h in range(2):
-                blk = jnp.where(c == h, last_own[...], last_in[...])
-                blk = jnp.where(c == 0, blk, pltpu.roll(blk, 64, 1))[:, :64]
-                dq_ref[:, 192 * h : 192 * (h + 1)] = blk[:192].T
-                do_ref[64 * h : 64 * (h + 1), :] = blk[192:]
-    dgain_ref[...] = sum_ref[7, 0:1]
-    dbias_ref[...] = sum_ref[7, 1:2]
-    for i in range(7):
-        sum_step(i, names[i]).wait_send()
+    sum_finish(BITS - 1)
+    sum_step(BITS).start()
+    sum_finish(BITS)
+    sums_ref[...] = sum_ref[BITS + 1]
+    store.wait()
+    final.wait()
+    for h in range(2):
+        blk = jnp.where(c == h, last_own[...], last_in[...])
+        last_ref[h] = jnp.where(c == 0, blk, pltpu.roll(blk, 64, 1))
+    for i in range(BITS + 1):
+        sum_step(i).wait_send()
     for k in range(COLOURS):
-        for bufs, sems in ((w_bufs, ag_send), (g_bufs, rs_send)):
+        for bufs, sems in ((w_bufs, ag_send), (g_bufs, rs_send_sem)):
             part = bufs[k].at[pl.ds(0, BLOCKS - 1)]
             pltpu.make_async_copy(part, part, sems.at[k]).wait()
 
 
+def finish(dtok_in, last_in, sums_in, dtok_ref, dq_ref, do_ref, dgain_ref, dbias_ref):
+    dtok_ref[...] = dtok_in[...]
+    for h in range(2):
+        blk = last_in[h].T[:64]
+        dq_ref[:, 192 * h : 192 * (h + 1)] = blk[:, :192]
+        do_ref[:, 64 * h : 64 * (h + 1)] = blk[:, 192:]
+    dgain_ref[...] = sums_in[0:1]
+    dbias_ref[...] = sums_in[1:2]
+
+
 def on_device(tokens, upstream, counts, norm_gain, norm_bias, w_qkv, w_out):
     vmem = pl.BlockSpec(memory_space=pltpu.VMEM)
+    hbm = pl.BlockSpec(memory_space=pltpu.HBM)
     blocks = [pltpu.VMEM((BLOCKS, r, 128), BF16) for r in ROWS]
     parts = [pltpu.VMEM((BLOCKS - 1, r, 128), BF16) for r in ROWS]
     dma = pltpu.SemaphoreType.DMA
-    outs = pl.pallas_call(
+    dtok, last, sums = pl.pallas_call(
         kernel,
         out_shape=(
             jax.ShapeDtypeStruct((256, D), BF16),
-            jax.ShapeDtypeStruct((64, 384), F32),
-            jax.ShapeDtypeStruct((128, 64), F32),
-            jax.ShapeDtypeStruct((1, D), F32),
-            jax.ShapeDtypeStruct((1, D), F32),
+            jax.ShapeDtypeStruct((2, 256, 128), F32),
+            jax.ShapeDtypeStruct((2, D), F32),
         ),
-        in_specs=[vmem, vmem, pl.BlockSpec(memory_space=pltpu.SMEM)] + [vmem] * 4,
-        out_specs=(vmem,) * 5,
+        in_specs=[hbm] * 7,
+        out_specs=(hbm, vmem, vmem),
         scratch_shapes=[
             *blocks,
             *blocks,
@@ -469,6 +505,15 @@
             dma((6,)),
             dma((7,)),
             dma((7,)),
+            pltpu.VMEM((256, D), BF16),
+            pltpu.VMEM((256, D), BF16),
+            pltpu.VMEM((64, 384), BF16),
+            pltpu.VMEM((64, 128), BF16),
+            pltpu.VMEM((1, D), F32),
+            pltpu.VMEM((1, D), F32),
+            pltpu.SMEM((32,), jnp.int32),
+            pltpu.VMEM((256, D), BF16),
+            dma((8,)),
         ],
         compiler_params=pltpu.CompilerParams(
             collective_id=0, has_side_effects=True, vmem_limit_bytes=60 * 1024 * 1024
@@ -480,10 +525,22 @@
         norm_gain.reshape(1, D),
         norm_bias.reshape(1, D),
         w_qkv,
-        w_out,
-    )
-    dtok, dq, do, dgain, dbias = outs
-    return dtok, dq, do, dgain.reshape(D), dbias.reshape(D)
+        w_out.T,
+    )
+    dtok, dq, do, dgain, dbias = pl.pallas_call(
+        finish,
+        out_shape=(
+            jax.ShapeDtypeStruct((256, D), BF16),
+            jax.ShapeDtypeStruct((64, 384), F32),
+            jax.ShapeDtypeStruct((64, 128), F32),
+            jax.ShapeDtypeStruct((1, D), F32),
+            jax.ShapeDtypeStruct((1, D), F32),
+        ),
+        in_specs=[vmem] * 3,
+        out_specs=(vmem,) * 5,
+        compiler_params=pltpu.CompilerParams(vmem_limit_bytes=60 * 1024 * 1024),
+    )(dtok, last, sums)
+    return dtok, dq, do.T, dgain.reshape(D), dbias.reshape(D)
 
 
 def solution(mesh):

time: 92.3 us -> 84 us (0.910)
  the two profiles are of different devices: /device:TPU:0 before, /device:TPU:1 now
where the time goes in v2:
time: 84 us; the launch traced here: 83.8 us
  Pallas kernels  83.2 us (99%)
    pallas_call x1, Pallas kernels, on_device(): pl.pallas_call(kernel, out_shape=(jax.ShapeDtypeStruct((256, D), BF16), j...  81.1 us
    pallas_call x1, Pallas kernels, on_device(): pl.pallas_call(finish, out_shape=(jax.ShapeDtypeStruct((256, D), BF16), j...  2.07 us

profile of v2, /device:TPU:1, one launch (start us, length us, event | category | flops | bytes accessed | tf_op | source)
XLA Modules:
  0.0 83.8 jit_solution(1594255468166057942)
XLA Ops:
  0.6 81.1 %shard_map.110 = (bf16[256,1024]{1,0:T(8,128)(2,1)}, f32[2,256,128]{2,1,0:T(8,128)}, f32[2,1024]{1,0:T(2,128)}) custom-call(bf16[256,1024]{1,0:T(8,128)(2,1)} %tok_in.1, bf16[256,1024]{1,0:T(8,128)(2,1)} %up_in.1, s32[32]{0:T(128)} %counts_in.1, f32[1,1024]{1,0:T(1,128)} %bitcast.7, f32[1,1024]{1,0:T(1,128)} %bitcast.8, bf16[64,384]{1,0:T(8,128)(2,1)} %wq_in.1, ...), custom_call_target="tpu_custom_call" | custom-call | tf_op jit(solution)/shard_map/pallas_call | solution.py:467
  81.8 2.1 %shard_map.111 = (bf16[256,1024]{1,0:T(8,128)(2,1)}, f32[64,384]{1,0:T(8,128)}, f32[64,128]{1,0:T(8,128)}, f32[1,1024]{1,0:T(1,128)}, f32[1,1024]{1,0:T(1,128)}) custom-call(bf16[256,1024]{1,0:T(8,128)(2,1)} %get-tuple-element.13.dtok_in, f32[2,256,128]{2,1,0:T(8,128)} %get-tuple-element.14.last_in, f32[2,1024]{1,0:T(2,128)} %get-tuple-element.15.sums_in), custom_call_target="tpu_custom_call" | custom-call | tf_op jit(solution)/shard_map/pallas_call | solution.py:530

commit v3 on v2

--- a/solution.py
+++ b/solution.py
@@ -51,22 +51,49 @@
     return total
 
 
-def held(bits, p):
+def held(bits, p, near):
     if p == 0:
         return joined(bits), 1
-    own = [0] * (p - 1) + [1 - bits[p - 1]] + list(bits[p:])
-    return joined(own), 1 << (p - 1)
+    if p == 1:
+        return joined([1 - bits[0]] + list(bits[1:])), 1
+    low = bits[p - 2] if near else 1 - bits[p - 2]
+    return joined([0] * (p - 2) + [low, 1 - bits[p - 1]] + list(bits[p:])), 1 << (p - 2)
+
+
+def kinds(p):
+    return (0, 1) if p > 1 else (0,)
 
 
 def across(bits, s):
     return list(bits[:s]) + [1 - bits[s]] + list(bits[s + 1 :])
 
 
-PIECE_AT = []
+PIECE_AT = {}
 _at = 0
 for _p in range(BITS):
-    PIECE_AT.append(_at)
-    _at += (BITS - _p) * max(1, (1 << _p) // 2)
+    for _near in kinds(_p):
+        PIECE_AT[_p, _near] = _at
+        _at += (BITS - _p) << max(0, _p - 2)
+
+EVENTS = [(BITS, 0)]
+for _p in range(BITS - 1, 0, -1):
+    EVENTS += [(_p, near) for near in kinds(_p)]
+
+
+def issue_event(s, p, near):
+    ready = 0 if s == BITS - 1 else EVENTS.index((s + 1, int(p < s)))
+    due = min(BITS, p + 1 if near else p + 2)
+    return max(ready, EVENTS.index((due, 0)))
+
+
+ISSUES = {event: [] for event in EVENTS}
+for _s in range(BITS):
+    for _p in range(_s, -1, -1):
+        for _near in kinds(_p):
+            ISSUES[EVENTS[issue_event(_s, _p, _near)]].append((_s, _p, _near))
+for _event in EVENTS:
+    ISSUES[_event].sort(key=lambda e: (e[0] != _event[0] - 1 or e[1] != e[0], -e[1], e[2]))
+
 BLOCKS = 1 << BITS
 
 
@@ -127,6 +154,10 @@
         bias_ref,
         counts_ref,
         dtok_ref,
+        score_ref,
+        gprob_ref,
+        key_ref,
+        pair_ref,
         load_sem,
     ) = scratch[18:]
 
@@ -194,24 +225,26 @@
     for k in range(COLOURS):
         w_bufs[k][joined(bits[k])] = block[FIRST[k] : FIRST[k] + ROWS[k]]
 
-    def ag_copy(k, s, p):
-        at, n = held(bits[k], p)
+    def ag_send_part(k, s, p, near):
+        at, n = held(bits[k], p, near)
         part = w_bufs[k].at[pl.ds(at, n)]
-        return remote(part, part, ag_send.at[k], ag_recv.at[k, s], order(k)[s])
-
-    def ag_sends(p):
+        sem = ag_recv.at[k, 2 * s + (p < s)]
+        remote(part, part, ag_send.at[k], sem, order(k)[s]).start()
+
+    def ag_event(p, near):
         for k in range(COLOURS):
             if p > 0:
-                at, n = held(bits[k], p)
+                at, n = held(bits[k], p, near)
                 part = w_bufs[k].at[pl.ds(at, n)]
-                pltpu.make_async_copy(part, part, ag_recv.at[k, p - 1]).wait()
+                sem = ag_recv.at[k, 2 * (p - 1) + near]
+                pltpu.make_async_copy(part, part, sem).wait()
             if p < BITS:
-                ag_copy(k, p, p).start()
+                ag_send_part(k, p, p, near)
         for s in range(p + 1, BITS):
             for k in range(COLOURS):
-                ag_copy(k, s, p).start()
-
-    ag_sends(0)
+                ag_send_part(k, s, p, near)
+
+    ag_event(0, 0)
 
     for load in loads[2:]:
         load.wait()
@@ -245,7 +278,8 @@
         copy.start()
 
     for p in range(1, BITS + 1):
-        ag_sends(p)
+        for near in kinds(p)[::-1]:
+            ag_event(p, near)
 
     def block_at(k, zz, yy, xx):
         return joined(bits_of(gray(xx, yy, zz), k))
@@ -286,34 +320,57 @@
 
     def unfolded(a):
         zero = jnp.zeros_like(a)
-        return jnp.concatenate([jnp.where(left, a, zero), jnp.where(left, zero, a)], axis=0).astype(
-            BF16
-        )
-
-    @pl.loop(0, 8)
+        both = [jnp.where(left, a, zero), jnp.where(left, zero, a)]
+        return jnp.concatenate(both, axis=0).astype(BF16)
+
+    pairs = [slice(128 * pair, 128 * pair + 128) for pair in range(4)]
+
+    @pl.loop(0, 8, unroll=4)
     def _(t):
         base = pl.multiple_of(t * 192, 192)
         o_base = pl.multiple_of(t * 64, 64)
-        for pair in range(4):
-            lanes = slice(pair * 128, pair * 128 + 128)
+        zero = jnp.zeros((64, 128), BF16)
+        for lanes in pairs:
             q = proj_ref[pl.ds(base, 64), lanes]
-            k = proj_ref[pl.ds(base + 64, 64), lanes]
-            v = proj_ref[pl.ds(base + 128, 64), lanes]
+            kv = proj_ref[pl.ds(base + 64, 128), lanes]
             g = gatt_ref[pl.ds(o_base, 64), lanes]
-            key_live = folded(live_ref[lanes, :]) > 0.5
-            scores = folded(dot(k, q, ((0,), (0,)))) * 0.125
-            scores = jnp.where(key_live, scores, -1e30)
-            top = jnp.max(scores, axis=0, keepdims=True)
-            powers = jnp.exp(scores - top)
-            probs = powers / jnp.sum(powers, axis=0, keepdims=True)
-            grad_probs = folded(dot(v, g, ((0,), (0,))))
-            delta = jnp.sum(probs * grad_probs, axis=0, keepdims=True)
-            grad_scores = unfolded(probs * (grad_probs - delta) * 0.125)
-            probs_low = unfolded(probs)
-            att_ref[pl.ds(o_base, 64), lanes] = dot(v, probs_low, ((1,), (0,))).astype(BF16)
-            gproj_ref[pl.ds(base, 64), lanes] = dot(k, grad_scores, ((1,), (0,))).astype(BF16)
-            gproj_ref[pl.ds(base + 64, 64), lanes] = dot(q, grad_scores, ((1,), (1,))).astype(BF16)
-            gproj_ref[pl.ds(base + 128, 64), lanes] = dot(g, probs_low, ((1,), (1,))).astype(BF16)
+            top = jnp.concatenate([q, zero], axis=1)
+            low = jnp.concatenate([zero, g], axis=1)
+            both = dot(kv, jnp.concatenate([top, low], axis=0), ((0,), (0,)))
+            score_ref[t, :, lanes] = folded(both[:, :128])
+            gprob_ref[t, :, lanes] = folded(both[:, 128:])
+
+    alive = [folded(live_ref[lanes, :]) for lanes in pairs]
+    key_ref[...] = jnp.concatenate(alive, axis=1)
+
+    @pl.loop(0, 8, unroll=2)
+    def _(t):
+        scores = jnp.where(key_ref[...] > 0.5, score_ref[t] * 0.125, -1e30)
+        powers = jnp.exp(scores - jnp.max(scores, axis=0, keepdims=True))
+        probs = powers * (1.0 / jnp.sum(powers, axis=0, keepdims=True))
+        grad_probs = gprob_ref[t]
+        delta = jnp.sum(probs * grad_probs, axis=0, keepdims=True)
+        grad_scores = probs * (grad_probs - delta) * 0.125
+        for i, lanes in enumerate(pairs):
+            pair_ref[t, i, :, 0:128] = unfolded(grad_scores[:, lanes])
+            pair_ref[t, i, :, 128:256] = unfolded(probs[:, lanes])
+
+
+    @pl.loop(0, 8, unroll=4)
+    def _(t):
+        base = pl.multiple_of(t * 192, 192)
+        o_base = pl.multiple_of(t * 64, 64)
+        for i, lanes in enumerate(pairs):
+            q = proj_ref[pl.ds(base, 64), lanes]
+            kv = proj_ref[pl.ds(base + 64, 128), lanes]
+            g = gatt_ref[pl.ds(o_base, 64), lanes]
+            out = dot(kv, pair_ref[t, i], ((1,), (0,))).astype(BF16)
+            gproj_ref[pl.ds(base, 64), lanes] = out[:64, :128]
+            att_ref[pl.ds(o_base, 64), lanes] = out[64:, 128:]
+            tall = jnp.concatenate([pair_ref[t, i, :, 0:128], pair_ref[t, i, :, 128:256]], axis=0)
+            out = dot(jnp.concatenate([q, g], axis=0), tall, ((1,), (1,))).astype(BF16)
+            gproj_ref[pl.ds(base + 64, 64), lanes] = out[:64, :128]
+            gproj_ref[pl.ds(base + 128, 64), lanes] = out[64:, 128:]
 
     swap = pair_copy(4, gn_out, gn_in)
     for other in (1, 0):
@@ -348,24 +405,29 @@
                     low = (yy % 2) * 192 + FIRST[k]
                     g_bufs[k][block_at(k, zz, yy, xx)] = out[low : low + 48, at : at + 128]
 
-    def q_part(k, p, s, count):
-        n = max(1, (1 << p) // 2)
-        return q_bufs[k].at[pl.ds(PIECE_AT[p] + (s - p) * n, count * n)]
-
-    def rs_send(k, s, p):
-        at, n = held(across(bits[k], s), p)
+    def q_part(k, p, near, s, count):
+        n = 1 << max(0, p - 2)
+        return q_bufs[k].at[pl.ds(PIECE_AT[p, near] + (s - p) * n, count * n)]
+
+    def rs_send(k, s, p, near):
+        at, n = held(across(bits[k], s), p, near)
         remote(
             g_bufs[k].at[pl.ds(at, n)],
-            q_part(k, p, s, 1),
+            q_part(k, p, near, s, 1),
             rs_send_sem.at[k],
-            rs_recv.at[k, p],
+            rs_recv.at[k, 2 * p + near],
             order(k)[s],
         ).start()
 
-    def rs_rest(s):
-        for p in range(s - 1, -1, -1):
-            for k in range(COLOURS):
-                rs_send(k, s, p)
+    def rs_wait(k, p, near):
+        whole = q_part(k, p, near, p, BITS - p)
+        pltpu.make_async_copy(whole, whole, rs_recv.at[k, 2 * p + near]).wait()
+
+    def rs_issue(event, ks, first):
+        for s, p, near in ISSUES[event]:
+            if (s == event[0] - 1 and p == s) == first:
+                for k in ks:
+                    rs_send(k, s, p, near)
 
     names = tuple(order(0)[::-1]) + ("c",)
 
@@ -388,9 +450,8 @@
         axis=0,
     )
     sum_step(0).start()
-    for k in range(COLOURS):
-        rs_send(k, BITS - 1, BITS - 1)
-    rs_rest(BITS - 1)
+    rs_issue((BITS, 0), range(COLOURS), True)
+    rs_issue((BITS, 0), range(COLOURS), False)
 
     live_own = live_ref[own_rows, :][:, :1]
     scaled = xhat_ref[...]
@@ -404,27 +465,24 @@
     store = pltpu.make_async_copy(dtok_ref, dtok_out, load_sem.at[7])
     store.start()
 
-    for s in range(BITS - 2, -1, -1):
-        p = s + 1
-        count = BITS - p
+    for event in EVENTS[1:]:
+        p, near = event
         for k in range(COLOURS):
-            at, n = held(bits[k], p)
-            whole = q_part(k, p, p, count)
-            pltpu.make_async_copy(whole, whole, rs_recv.at[k, p]).wait()
+            rs_wait(k, p, near)
+            at, n = held(bits[k], p, near)
             total = g_bufs[k][pl.ds(at, n)].astype(F32)
-            for j in range(count):
-                first_at = PIECE_AT[p] + j * n
+            for j in range(BITS - p):
+                first_at = PIECE_AT[p, near] + j * n
                 total = total + q_bufs[k][first_at : first_at + n].astype(F32)
             g_bufs[k][pl.ds(at, n)] = total.astype(BF16)
-            if k == 0:
-                i = BITS - 2 - s
+            if k == 0 and near == 0:
+                i = BITS - 1 - p
                 sum_finish(i)
                 sum_step(i + 1).start()
-            rs_send(k, s, s)
-        rs_rest(s)
+            rs_issue(event, (k,), True)
+        rs_issue(event, range(COLOURS), False)
     for k in range(COLOURS):
-        whole = q_part(k, 0, 0, BITS)
-        pltpu.make_async_copy(whole, whole, rs_recv.at[k, 0]).wait()
+        rs_wait(k, 0, 0)
         total = g_bufs[k][joined(bits[k])].astype(F32)
         for s in range(BITS):
             total = total + q_bufs[k][s].astype(F32)
@@ -498,9 +556,9 @@
             pltpu.VMEM((256, 128), F32),
             pltpu.VMEM((256, 128), F32),
             dma((COLOURS,)),
-            dma((COLOURS, BITS)),
+            dma((COLOURS, 2 * BITS)),
             dma((COLOURS,)),
-            dma((COLOURS, BITS)),
+            dma((COLOURS, 2 * BITS)),
             dma((6,)),
             dma((6,)),
             dma((7,)),
@@ -513,6 +571,10 @@
             pltpu.VMEM((1, D), F32),
             pltpu.SMEM((32,), jnp.int32),
             pltpu.VMEM((256, D), BF16),
+            pltpu.VMEM((8, 64, 512), F32),
+            pltpu.VMEM((8, 64, 512), F32),
+            pltpu.VMEM((64, 512), F32),
+            pltpu.VMEM((8, 4, 128, 256), BF16),
             dma((8,)),
         ],
         compiler_params=pltpu.CompilerParams(

time: 84 us -> 73.1 us (0.87)
  Pallas kernels: 83.2 us -> 72.4 us
    pallas_call x1, Pallas kernels: 81.1 us -> 70.3 us  [on_device(): pl.pallas_call(kernel, out_shape=(jax.ShapeDtypeStruct((256, D), BF16), j...]
where the time goes in v3:
time: 73.1 us; the launch traced here: 73 us
  Pallas kernels  72.4 us (99%)
    pallas_call x1, Pallas kernels, on_device(): pl.pallas_call(kernel, out_shape=(jax.ShapeDtypeStruct((256, D), BF16), j...  70.3 us
    pallas_call x1, Pallas kernels, on_device(): pl.pallas_call(finish, out_shape=(jax.ShapeDtypeStruct((256, D), BF16), j...  2.07 us

profile of v3, /device:TPU:1, one launch (start us, length us, event | category | flops | bytes accessed | tf_op | source)
XLA Modules:
  0.0 73.0 jit_solution(15332627201368855676)
XLA Ops:
  0.6 70.3 %shard_map.110 = (bf16[256,1024]{1,0:T(8,128)(2,1)}, f32[2,256,128]{2,1,0:T(8,128)}, f32[2,1024]{1,0:T(2,128)}) custom-call(bf16[256,1024]{1,0:T(8,128)(2,1)} %tok_in.1, bf16[256,1024]{1,0:T(8,128)(2,1)} %up_in.1, s32[32]{0:T(128)} %counts_in.1, f32[1,1024]{1,0:T(1,128)} %bitcast.7, f32[1,1024]{1,0:T(1,128)} %bitcast.8, bf16[64,384]{1,0:T(8,128)(2,1)} %wq_in.1, ...), custom_call_target="tpu_custom_call" | custom-call | tf_op jit(solution)/shard_map/pallas_call | solution.py:525
  70.9 2.1 %shard_map.111 = (bf16[256,1024]{1,0:T(8,128)(2,1)}, f32[64,384]{1,0:T(8,128)}, f32[64,128]{1,0:T(8,128)}, f32[1,1024]{1,0:T(1,128)}, f32[1,1024]{1,0:T(1,128)}) custom-call(bf16[256,1024]{1,0:T(8,128)(2,1)} %get-tuple-element.13.dtok_in, f32[2,256,128]{2,1,0:T(8,128)} %get-tuple-element.14.last_in, f32[2,1024]{1,0:T(2,128)} %get-tuple-element.15.sums_in), custom_call_target="tpu_custom_call" | custom-call | tf_op jit(solution)/shard_map/pallas_call | solution.py:592
